TPU v7x, 32 devices: a whole 2x2x4 slice. The times are simulated.
32 devices in a mesh: expert: 8 (over z, core), row: 4 (over y, x).
Axes of the slice: x: 2, y: 2, z: 4, core: 2. Of those that a mesh axis runs over, the one named last changes fastest.
Arguments:
- grads: bfloat16 [8, 7168, 2048], P('expert', 'row')
- basis: bfloat16 [8, 7168, 256], P('expert', 'row'), may hold values from -0.0625 to 0.0625
- loads: int32 [8], P('expert'), may hold values from 1 to 1, as said below
- flags: int32 [8], P('expert'), may hold values 0 or 1
Outputs:
- new_basis: float32 [8, 7168, 256], P('expert', 'row')
- rotated: float32 [8, 256, 2048], P('expert', None, 'row')
Inputs may be any that keep to these rules, and one draw needn't show every extreme that they name: Slots 0 to loads[d] - 1 of expert-axis index d are live and hold experts; the others are empty. Some index has all 1 slots live.
All inputs are finite; a program needn't handle non-finite values. No bound on the sum of `flags` on one device may be relied on, other than what follows from the above.
Results may differ from a plain program's by a relative error of at most 0.006.
Values sent between devices are 32-bit elements; how exact they have to be, the bound alone decides.
A program may use at most 64 MiB of HBM per device.

v0:
```python
import jax
import jax.numpy as jnp
from jax import lax
from jax.sharding import PartitionSpec as P

D = 7168
S = 2048


def on_device(grads, basis, loads, flags):
    slot_count = grads.shape[0]
    live_count = loads[0]
    live_mask = jnp.arange(slot_count, dtype=jnp.int32) < live_count
    refresh = jnp.logical_and(live_mask, flags == 1)
    live_cube = live_mask[:, None, None]
    refresh_cube = refresh[:, None, None]
    squares = jnp.sum(jnp.where(live_cube, jnp.square(grads.astype(jnp.float32)), 0.0))
    leader = (lax.axis_index("row") == 0).astype(jnp.float32)
    total_sq, total_live = lax.psum(
        (squares, leader * live_count.astype(jnp.float32)), ("expert", "row")
    )
    norm_scale = lax.rsqrt(total_sq / (total_live * D * S) + 1e-06)
    local_inner = jnp.einsum("cds,cdk->csk", grads, basis, preferred_element_type=jnp.float32)
    inner_sum = jnp.stack([lax.psum(local_inner[0], "row")])
    inner_gram = jnp.einsum("csk,csj->ckj", inner_sum, inner_sum, precision=lax.Precision.HIGHEST)
    inner_half = inner_sum.astype(jnp.bfloat16)
    power_rows = jnp.einsum(
        "cds,csk->cdk", grads, inner_half, preferred_element_type=jnp.float32
    ).astype(jnp.bfloat16)
    projector = jnp.where(refresh_cube, power_rows, basis)
    local_cross = jnp.einsum("cdk,cds->cks", projector, grads, preferred_element_type=jnp.float32)
    identity = jnp.eye(basis.shape[2], dtype=jnp.float32)
    lower_first = jnp.linalg.cholesky(jnp.where(refresh_cube, inner_gram, identity))
    first_rows = lax.linalg.triangular_solve(
        lower_first, power_rows.astype(jnp.float32), left_side=False, lower=True, transpose_a=True
    )
    local_second = jnp.einsum(
        "cdk,cdj->ckj", first_rows, first_rows, precision=lax.Precision.HIGHEST
    )
    gram_again = lax.psum(local_second, "row")
    cross_cols = lax.psum_scatter(local_cross, "row", scatter_dimension=2, tiled=True)
    lower_second = jnp.linalg.cholesky(jnp.where(refresh_cube, gram_again, identity))
    fresh_basis = lax.linalg.triangular_solve(
        lower_second, first_rows, left_side=False, lower=True, transpose_a=True
    )
    half_solved = lax.linalg.triangular_solve(lower_first, cross_cols, left_side=True, lower=True)
    fresh_rot = lax.linalg.triangular_solve(lower_second, half_solved, left_side=True, lower=True)
    new_basis = jnp.where(
        refresh_cube, fresh_basis, jnp.where(live_cube, basis.astype(jnp.float32), 0.0)
    )
    rotated = jnp.where(refresh_cube, fresh_rot, jnp.where(live_cube, cross_cols, 0.0)) * norm_scale
    return (new_basis, rotated)


def solution(mesh):
    placed = (P("expert", "row", None), P("expert", "row", None), P("expert"), P("expert"))
    return jax.shard_map(
        on_device,
        mesh=mesh,
        in_specs=placed,
        out_specs=(P("expert", "row", None), P("expert", None, "row")),
        check_vma=False,
    )
```

profile of v0, /device:TPU:0, one launch (start us, length us, event | category | flops | bytes accessed | tf_op | source)
XLA Modules:
  0.0 307.3 jit_solution(6141670956639925859)
XLA Ops:
  7.2 6.8 %fusion.4 = f32[2048,256]{1,0:T(8,128)} fusion(bf16[1,1792,2048]{2,1,0:T(8,128)(2,1)} %param.9, bf16[1,1792,256]{2,1,0:T(8,128)(2,1)} %param.10), kind=kOutput, calls=%fused_computation.9 | convolution fusion | flops 1879048192 | bytes 10354688 | tf_op jit(solution)/shard_map/cds,cdk->csk/dot_general | solution.py:23
  14.1 1.1 copy-done.2
  15.2 1.1 copy.12
  17.7 68.7 %all-reduce.5.cloned.1.call-done = f32[2048,256]{1,0:T(8,128)} async-done(((f32[2048,256]{1,0:T(8,128)}), f32[2048,256]{1,0:T(8,128)}) %all-reduce.5.cloned.1.call-update) | async-done | bytes 2097168 | tf_op jit(solution)/shard_map/psum | solution.py:24
  86.4 5.7 %convolution_select_fusion = f32[256,256]{0,1:T(8,128)S(1)} fusion(f32[2048,256]{1,0:T(8,128)} %all-reduce.5.cloned.1.call-done, pred[]{:T(512)} %bitcast), kind=kOutput, calls=%fused_computation.32 | convolution fusion | flops 1610809344 | bytes 2359297 | tf_op jit(solution)/shard_map/csk,csj->ckj/dot_general | solution.py:25
  93.0 11.7 %custom-call.21 = f32[1,128,128]{2,1,0:T(8,128)S(1)} custom-call(f32[1,128,128]{2,1,0:T(8,128)S(1)} %cholesky.191), custom_call_target="Cholesky" | custom-call | tf_op jit(solution)/shard_map/jit(cholesky)/cholesky | solution.py:33
  104.7 9.8 %custom-call.22 = f32[1,1,128,128]{2,3,1,0:T(8,128)S(1)} custom-call(f32[1,1,128,128]{3,2,1,0:T(8,128)S(1)} %get-tuple-element.68), custom_call_target="InvertDiagBlocksLowerTriangular" | custom-call | tf_op jit(solution)/shard_map/jit(cholesky)/cholesky | solution.py:33
  114.6 1.0 bitcast_dynamic-update-slice_fusion.3
  115.6 1.1 fusion.27
  116.7 11.9 %custom-call.23 = f32[1,128,128]{2,1,0:T(8,128)S(1)} custom-call(f32[1,128,128]{2,1,0:T(8,128)S(1)} %fusion.27), custom_call_target="Cholesky" | custom-call | tf_op jit(solution)/shard_map/jit(cholesky)/cholesky | solution.py:33
  130.7 3.9 %while.8 = (s32[]{:T(128)}, f32[1,256,256]{2,1,0:T(8,128)S(1)}, s32[2,2]{1,0:T(2,128)S(1)}, f32[2,1,128,128]{3,2,1,0:T(8,128)S(1)}, s32[]{:T(128)}) while((s32[]{:T(128)}, f32[1,256,256]{2,1,0:T(8,128)S(1)}, s32[2,2]{1,0:T(2,128)S(1)}, f32[2,1,128,128]{3,2,1,0:T(8,128)S(1)}, s32[]{:T(128)}) %tuple.57), condition=%wide.while_cond, body=%wide.while_body.sunk | while | flops 2 | bytes 131181 | solution.py:34
  131.3 1.4 bitcast_dynamic-update-slice_fusion.6
  133.3 1.4 bitcast_dynamic-update-slice_fusion.6
  134.6 19.7 %custom-call.24 = f32[1,2,128,128]{2,3,1,0:T(8,128)S(1)} custom-call(f32[1,2,128,128]{3,2,1,0:T(8,128)S(1)} %bitcast.221), custom_call_target="InvertDiagBlocksLowerTriangular" | custom-call | tf_op jit(solution)/shard_map/triangular_solve/custom-call.0 | solution.py:34
  154.3 6.2 %fusion.53 = (f32[1,1792,256]{1,2,0:T(8,128)S(1)}, bf16[1,1792,256]{1,2,0:T(8,128)(2,1)}) fusion(bf16[1,1792,2048]{2,1,0:T(8,128)(2,1)} %param.9, f32[2048,256]{1,0:T(8,128)S(1)} %copy-done), kind=kOutput, calls=%fused_computation.99 | convolution fusion | flops 1880489984 | bytes 12189696 | tf_op jit(solution)/shard_map/cds,csk->cdk/dot_general | solution.py:27
  163.4 2.4 fusion.22
  165.9 6.8 %fusion.6 = f32[1,256,2048]{2,1,0:T(8,128)} fusion(bf16[1,1792,2048]{2,1,0:T(8,128)(2,1)} %param.9, bf16[1,1792,256]{1,2,0:T(8,128)(2,1)} %get-tuple-element.70, bf16[1,1792,256]{1,2,0:T(8,128)(2,1)S(1)} %copy.12, pred[]{:T(512)} %bitcast), kind=kOutput, calls=%fused_computation.11 | convolution fusion | flops 1879506944 | bytes 11272193 | tf_op jit(solution)/shard_map/cdk,cds->cks/dot_general | solution.py:31
  172.7 7.5 %select_reduce_fusion = f32[]{:T(128)} fusion(bf16[1,1792,2048]{2,1,0:T(8,128)(2,1)} %param.9, pred[]{:T(512)} %bitcast.40), kind=kLoop, calls=%fused_computation.4 | loop fusion | flops 14680063 | bytes 7340037 | tf_op jit(solution)/shard_map/reduce_sum | solution.py:17
  180.2 39.4 %all-reduce.1 = (f32[]{:T(128)}, f32[]{:T(128)}) all-reduce(f32[]{:T(128)} %select_reduce_fusion, f32[]{:T(128)S(6)} %mul.13), channel_id=1, replica_groups=mesh['expert'=8,'row'=4] {'expert','row'}, use_global_device_ids=true, to_apply=%region_8.12 | all-reduce | flops 2 | bytes 16 | tf_op jit(solution)/shard_map/psum | solution.py:19
  222.1 1.0 fusion.40
  223.1 12.3 %custom-call.25 = f32[1,128,128]{2,1,0:T(8,128)} custom-call(f32[1,128,128]{2,1,0:T(8,128)S(1)} %cholesky.194), custom_call_target="Cholesky" | custom-call | tf_op jit(solution)/shard_map/jit(cholesky)/cholesky | solution.py:42
  236.3 1.5 select_reduce_fusion.2
  237.8 11.3 %custom-call.26 = f32[1,1,128,128]{2,3,1,0:T(8,128)} custom-call(f32[1,1,128,128]{3,2,1,0:T(8,128)} %get-tuple-element.64), custom_call_target="InvertDiagBlocksLowerTriangular" | custom-call | tf_op jit(solution)/shard_map/jit(cholesky)/cholesky | solution.py:42
  249.1 1.0 bitcast_dynamic-update-slice_fusion.2
  251.1 12.5 %custom-call.27 = f32[1,128,128]{2,1,0:T(8,128)S(1)} custom-call(f32[1,128,128]{2,1,0:T(8,128)} %fusion.28), custom_call_target="Cholesky" | custom-call | tf_op jit(solution)/shard_map/jit(cholesky)/cholesky | solution.py:42
  266.3 4.0 %while.9 = (s32[]{:T(128)}, f32[1,256,256]{2,1,0:T(8,128)S(1)}, s32[2,2]{1,0:T(2,128)S(1)}, f32[2,1,128,128]{3,2,1,0:T(8,128)S(1)}, s32[]{:T(128)}) while((s32[]{:T(128)}, f32[1,256,256]{2,1,0:T(8,128)S(1)}, s32[2,2]{1,0:T(2,128)S(1)}, f32[2,1,128,128]{3,2,1,0:T(8,128)S(1)}, s32[]{:T(128)}) %tuple.69), condition=%wide.while_cond.clone, body=%wide.while_body.clone.sunk | while | flops 2 | bytes 131181 | solution.py:43
  266.9 1.4 bitcast_dynamic-update-slice_fusion.7
  268.9 1.4 bitcast_dynamic-update-slice_fusion.7
  270.3 19.9 %custom-call.28 = f32[1,2,128,128]{2,3,1,0:T(8,128)S(1)} custom-call(f32[1,2,128,128]{3,2,1,0:T(8,128)S(1)} %bitcast.220), custom_call_target="InvertDiagBlocksLowerTriangular" | custom-call | tf_op jit(solution)/shard_map/triangular_solve/custom-call.0 | solution.py:43
  293.3 1.7 copy.14
  295.0 1.4 fusion.38
  297.3 1.3 fusion.24
  (60 shorter events, 17.0 us)
Async XLA Ops:
  7.2 79.2 %all-reduce.5.cloned.1.call-start = ((), (), s32[]{:S(2)}) async-start(), calls=%async_computation.1 | async-start | bytes 4194304 | tf_op jit(solution)/shard_map/psum | solution.py:24
  14.0 1.2 copy-start.2
  14.1 206.9 %all-reduce.7.cloned.1.call-start = ((), (), s32[]{:S(2)}) async-start(), calls=%async_computation.2 | async-start | bytes 524288 | tf_op jit(solution)/shard_map/psum | solution.py:40
  92.1 62.3 %copy-start = (f32[2048,256]{1,0:T(8,128)S(1)}, f32[2048,256]{1,0:T(8,128)}, u32[]{:S(2)}) copy-start(f32[2048,256]{1,0:T(8,128)} %all-reduce.5.cloned.1.call-done) | copy-start | bytes 6291460
  92.3 0.7 copy-start.3
  154.3 8.1 %copy-start.4 = (f32[1,2,128,128]{2,3,1,0:T(8,128)}, f32[1,2,128,128]{2,3,1,0:T(8,128)S(1)}, u32[]{:S(2)}) copy-start(f32[1,2,128,128]{2,3,1,0:T(8,128)S(1)} %custom-call.24) | copy-start | bytes 393220
  165.8 129.2 %reduce-scatter.2.cloned.1.call-start = ((), (), s32[]{:S(2)}) async-start(), calls=%async_computation.3 | async-start | bytes 2621440 | tf_op jit(solution)/shard_map/reduce_scatter | solution.py:41
  293.3 1.7 copy-start.5
  295.0 4.4 %copy-start.1 = (f32[1,256,512]{2,1,0:T(8,128)S(1)}, f32[1,256,512]{2,1,0:T(8,128)}, u32[]{:S(2)}) copy-start(f32[1,256,512]{2,1,0:T(8,128)} %reduce-scatter.2.cloned.1.call-done) | copy-start | bytes 1572868
Sparse Core Ops, SparseCore 0:
  14.2 72.1 all-reduce.4
  165.9 43.0 all-reduce.6
  211.9 35.2 reduce-scatter.1
where the time goes:
time: 311 us; the launch traced here: 307 us
  other arithmetic  123 us (40%)
  waiting for transfers between devices  68.8 us (22%)
  matrix products  42 us (14%)
  blocking collectives  39.4 us (13%)
  between operations  19.7 us (6%)
  local copies, waits for them, and re-layouts  13.7 us (4%)
    psum x1, waiting for transfers between devices, on_device(): inner_sum = jnp.stack([lax.psum(local_inner[0], 'row')])  68.7 us
    psum x1, blocking collectives, on_device(): lax.psum((squares, leader * live_count.astype(jnp.float32)), ('expert', '...  39.4 us
    another operation x7, other arithmetic, on_device(): jnp.linalg.cholesky(jnp.where(refresh_cube, gram_again, identity))  39 us
    another operation x6, other arithmetic, on_device(): jnp.linalg.cholesky(jnp.where(refresh_cube, inner_gram, identity))  34.1 us
    another operation x2, other arithmetic, on_device(): lax.linalg.triangular_solve(lower_second, first_rows, left_side=False, lo...  20 us
    another operation x3, other arithmetic, on_device(): lax.linalg.triangular_solve(lower_first, power_rows.astype(jnp.float32),...  19.7 us
    reduce_sum x1, other arithmetic, on_device(): jnp.sum(jnp.where(live_cube, jnp.square(grads.astype(jnp.float32)), 0.0))  7.48 us
    dot_general x1, matrix products, on_device(): jnp.einsum('cds,cdk->csk', grads, basis, preferred_element_type=jnp.float32)  6.82 us
  transfers between devices with their start and end apart: 3, of which 1 were waited for; matrix products, arithmetic and copies ran while one was open for 29% of the time, Pallas kernels for 0%

commit v1 on v0

--- a/solution.py
+++ b/solution.py
@@ -5,6 +5,11 @@
 
 D = 7168
 S = 2048
+
+
+def summed_here(x, name):
+    terms = lax.all_gather(x, name)
+    return jnp.sum(terms, axis=0)
 
 
 def on_device(grads, basis, loads, flags):
@@ -21,7 +26,7 @@
     )
     norm_scale = lax.rsqrt(total_sq / (total_live * D * S) + 1e-06)
     local_inner = jnp.einsum("cds,cdk->csk", grads, basis, preferred_element_type=jnp.float32)
-    inner_sum = jnp.stack([lax.psum(local_inner[0], "row")])
+    inner_sum = jnp.stack([summed_here(local_inner[0], "row")])
     inner_gram = jnp.einsum("csk,csj->ckj", inner_sum, inner_sum, precision=lax.Precision.HIGHEST)
     inner_half = inner_sum.astype(jnp.bfloat16)
     power_rows = jnp.einsum(

time: 311 us -> 332 us (1.068)
  waiting for transfers between devices: 68.8 us -> 87.2 us
  other arithmetic: 123 us -> 128 us
    all_gather x0 -> x1, waiting for transfers between devices: none -> 87.1 us  [summed_here(): terms = lax.all_gather(x, name)]
    psum x1 -> x0, waiting for transfers between devices: 68.7 us -> none  [on_device(): inner_sum = jnp.stack([lax.psum(local_inner[0], 'row')])]
    reduce_sum x0 -> x1, other arithmetic: none -> 4.21 us  [summed_here(): return jnp.sum(terms, axis=0)]
  transfers between devices with their start and end apart: 3 -> 3, of which waited for: 1 -> 1; matrix products, arithmetic and copies ran while one was open for 29% -> 27% of each run, Pallas kernels for 0% -> 0%
where the time goes in v1:
time: 332 us; the launch traced here: 328 us
  other arithmetic  128 us (39%)
  waiting for transfers between devices  87.2 us (26%)
  matrix products  41.3 us (12%)
  blocking collectives  39.2 us (12%)
  between operations  19.5 us (6%)
  local copies, waits for them, and re-layouts  12.8 us (4%)
    all_gather x1, waiting for transfers between devices, summed_here(): terms = lax.all_gather(x, name)  87.1 us
    psum x1, blocking collectives, on_device(): lax.psum((squares, leader * live_count.astype(jnp.float32)), ('expert', '...  39.2 us
    another operation x7, other arithmetic, on_device(): jnp.linalg.cholesky(jnp.where(refresh_cube, gram_again, identity))  39 us
    another operation x6, other arithmetic, on_device(): jnp.linalg.cholesky(jnp.where(refresh_cube, inner_gram, identity))  34.4 us
    another operation x2, other arithmetic, on_device(): lax.linalg.triangular_solve(lower_second, first_rows, left_side=False, lo...  19.9 us
    another operation x3, other arithmetic, on_device(): lax.linalg.triangular_solve(lower_first, power_rows.astype(jnp.float32),...  19.7 us
    reduce_sum x1, other arithmetic, on_device(): jnp.sum(jnp.where(live_cube, jnp.square(grads.astype(jnp.float32)), 0.0))  7.49 us
    dot_general x1, matrix products, on_device(): jnp.einsum('cds,cdk->csk', grads, basis, preferred_element_type=jnp.float32)  6.97 us
  transfers between devices with their start and end apart: 3, of which 1 were waited for; matrix products, arithmetic and copies ran while one was open for 27% of the time, Pallas kernels for 0%

profile of v1, /device:TPU:0, one launch (start us, length us, event | category | flops | bytes accessed | tf_op | source)
XLA Modules:
  0.0 328.2 jit_solution(1827397809790140574)
XLA Ops:
  7.2 7.0 %fusion.4 = f32[2048,256]{1,0:T(8,128)} fusion(bf16[1,1792,2048]{2,1,0:T(8,128)(2,1)} %param.9, bf16[1,1792,256]{2,1,0:T(8,128)(2,1)} %param.10), kind=kOutput, calls=%fused_computation.9 | convolution fusion | flops 1879048192 | bytes 10354688 | tf_op jit(solution)/shard_map/cds,cdk->csk/dot_general | solution.py:28
  14.3 1.1 copy-done.1
  17.5 87.1 %all-gather.3.cloned.1.call-done = f32[8192,256]{1,0:T(8,128)} async-done(((f32[2048,256]{1,0:T(8,128)}), f32[8192,256]{1,0:T(8,128)}) %all-gather.3.cloned.1.call-update) | async-done | bytes 8388624 | tf_op jit(solution)/shard_map/all_gather | solution.py:11
  104.6 4.2 %reduce_sum.18 = f32[2048,256]{1,0:T(8,128)S(1)} reduce(f32[4,2048,256]{2,1,0:T(8,128)} %bitcast.217, f32[]{:T(128)} %constant.80.clone.1), dimensions={0}, to_apply=%region_0.1 | reduce | flops 1572864 | bytes 10485764 | tf_op jit(solution)/shard_map/reduce_sum | solution.py:12
  108.8 6.8 %fusion.53 = (f32[1,1792,256]{1,2,0:T(8,128)}, bf16[1,1792,256]{1,2,0:T(8,128)(2,1)}) fusion(bf16[1,1792,2048]{2,1,0:T(8,128)(2,1)} %param.9, f32[2048,256]{1,0:T(8,128)S(1)} %reduce_sum.18), kind=kOutput, calls=%fused_computation.99 | convolution fusion | flops 1880489984 | bytes 12189696 | tf_op jit(solution)/shard_map/cds,csk->cdk/dot_general | solution.py:32
  115.5 3.4 %convolution_select_fusion = f32[256,256]{0,1:T(8,128)S(1)} fusion(f32[2048,256]{1,0:T(8,128)S(1)} %reduce_sum.18, pred[]{:T(512)} %bitcast), kind=kOutput, calls=%fused_computation.32 | convolution fusion | flops 1610809344 | bytes 2359297 | tf_op jit(solution)/shard_map/csk,csj->ckj/dot_general | solution.py:30
  119.2 11.7 %custom-call.21 = f32[1,128,128]{2,1,0:T(8,128)S(1)} custom-call(f32[1,128,128]{2,1,0:T(8,128)S(1)} %cholesky.191), custom_call_target="Cholesky" | custom-call | tf_op jit(solution)/shard_map/jit(cholesky)/cholesky | solution.py:38
  131.0 10.2 %custom-call.22 = f32[1,1,128,128]{2,3,1,0:T(8,128)S(1)} custom-call(f32[1,1,128,128]{3,2,1,0:T(8,128)S(1)} %get-tuple-element.68), custom_call_target="InvertDiagBlocksLowerTriangular" | custom-call | tf_op jit(solution)/shard_map/jit(cholesky)/cholesky | solution.py:38
  141.6 11.7 %custom-call.23 = f32[1,128,128]{2,1,0:T(8,128)S(1)} custom-call(f32[1,128,128]{2,1,0:T(8,128)S(1)} %fusion.27), custom_call_target="Cholesky" | custom-call | tf_op jit(solution)/shard_map/jit(cholesky)/cholesky | solution.py:38
  155.5 4.1 %while.8 = (s32[]{:T(128)}, f32[1,256,256]{2,1,0:T(8,128)S(1)}, s32[2,2]{1,0:T(2,128)S(1)}, f32[2,1,128,128]{3,2,1,0:T(8,128)S(1)}, s32[]{:T(128)}) while((s32[]{:T(128)}, f32[1,256,256]{2,1,0:T(8,128)S(1)}, s32[2,2]{1,0:T(2,128)S(1)}, f32[2,1,128,128]{3,2,1,0:T(8,128)S(1)}, s32[]{:T(128)}) %tuple.57), condition=%wide.while_cond, body=%wide.while_body.sunk | while | flops 2 | bytes 131189 | solution.py:39
  156.2 1.3 bitcast_dynamic-update-slice_fusion.6
  158.2 1.3 bitcast_dynamic-update-slice_fusion.6
  159.6 19.7 %custom-call.24 = f32[1,2,128,128]{2,3,1,0:T(8,128)S(1)} custom-call(f32[1,2,128,128]{3,2,1,0:T(8,128)S(1)} %bitcast.223), custom_call_target="InvertDiagBlocksLowerTriangular" | custom-call | tf_op jit(solution)/shard_map/triangular_solve/custom-call.0 | solution.py:39
  179.3 2.2 fusion.30
  181.4 2.1 fusion.16
  184.5 2.4 fusion.22
  187.2 6.8 %fusion.6 = f32[1,256,2048]{2,1,0:T(8,128)} fusion(bf16[1,1792,2048]{2,1,0:T(8,128)(2,1)} %param.9, bf16[1,1792,256]{1,2,0:T(8,128)(2,1)} %get-tuple-element.70, bf16[1,1792,256]{1,2,0:T(8,128)(2,1)S(1)} %copy.12, pred[]{:T(512)} %bitcast), kind=kOutput, calls=%fused_computation.11 | convolution fusion | flops 1879506944 | bytes 11272193 | tf_op jit(solution)/shard_map/cdk,cds->cks/dot_general | solution.py:36
  194.0 7.5 %select_reduce_fusion = f32[]{:T(128)} fusion(bf16[1,1792,2048]{2,1,0:T(8,128)(2,1)} %param.9, pred[]{:T(512)} %bitcast.41), kind=kLoop, calls=%fused_computation.4 | loop fusion | flops 14680063 | bytes 7340037 | tf_op jit(solution)/shard_map/reduce_sum | solution.py:22
  201.5 39.2 %all-reduce.1 = (f32[]{:T(128)}, f32[]{:T(128)}) all-reduce(f32[]{:T(128)} %select_reduce_fusion, f32[]{:T(128)S(6)} %mul.13), channel_id=1, replica_groups=mesh['expert'=8,'row'=4] {'expert','row'}, use_global_device_ids=true, to_apply=%region_8.12 | all-reduce | flops 2 | bytes 16 | tf_op jit(solution)/shard_map/psum | solution.py:24
  243.2 1.0 fusion.40
  244.2 12.3 %custom-call.25 = f32[1,128,128]{2,1,0:T(8,128)} custom-call(f32[1,128,128]{2,1,0:T(8,128)S(1)} %cholesky.194), custom_call_target="Cholesky" | custom-call | tf_op jit(solution)/shard_map/jit(cholesky)/cholesky | solution.py:47
  257.4 1.5 select_reduce_fusion.2
  258.9 11.3 %custom-call.26 = f32[1,1,128,128]{2,3,1,0:T(8,128)} custom-call(f32[1,1,128,128]{3,2,1,0:T(8,128)} %get-tuple-element.64), custom_call_target="InvertDiagBlocksLowerTriangular" | custom-call | tf_op jit(solution)/shard_map/jit(cholesky)/cholesky | solution.py:47
  270.2 1.0 bitcast_dynamic-update-slice_fusion.2
  272.2 12.5 %custom-call.27 = f32[1,128,128]{2,1,0:T(8,128)S(1)} custom-call(f32[1,128,128]{2,1,0:T(8,128)} %fusion.28), custom_call_target="Cholesky" | custom-call | tf_op jit(solution)/shard_map/jit(cholesky)/cholesky | solution.py:47
  287.4 4.0 %while.9 = (s32[]{:T(128)}, f32[1,256,256]{2,1,0:T(8,128)S(1)}, s32[2,2]{1,0:T(2,128)S(1)}, f32[2,1,128,128]{3,2,1,0:T(8,128)S(1)}, s32[]{:T(128)}) while((s32[]{:T(128)}, f32[1,256,256]{2,1,0:T(8,128)S(1)}, s32[2,2]{1,0:T(2,128)S(1)}, f32[2,1,128,128]{3,2,1,0:T(8,128)S(1)}, s32[]{:T(128)}) %tuple.69), condition=%wide.while_cond.clone, body=%wide.while_body.clone.sunk | while | flops 2 | bytes 131189 | solution.py:48
  288.0 1.4 bitcast_dynamic-update-slice_fusion.7
  290.0 1.4 bitcast_dynamic-update-slice_fusion.7
  291.4 19.9 %custom-call.28 = f32[1,2,128,128]{2,3,1,0:T(8,128)S(1)} custom-call(f32[1,2,128,128]{3,2,1,0:T(8,128)S(1)} %bitcast.222), custom_call_target="InvertDiagBlocksLowerTriangular" | custom-call | tf_op jit(solution)/shard_map/triangular_solve/custom-call.0 | solution.py:48
  314.4 1.7 copy.14
  316.1 1.4 fusion.38
  318.3 1.3 fusion.24
  (57 shorter events, 16.0 us)
Async XLA Ops:
  7.2 97.4 %all-gather.3.cloned.1.call-start = ((), (), s32[]{:S(2)}) async-start(), calls=%async_computation.3 | async-start | bytes 10485760 | tf_op jit(solution)/shard_map/all_gather | solution.py:11
  14.2 1.2 copy-start.1
  14.2 227.8 %all-reduce.4.cloned.1.call-start = ((), (), s32[]{:S(2)}) async-start(), calls=%async_computation.1 | async-start | bytes 524288 | tf_op jit(solution)/shard_map/psum | solution.py:45
  179.3 4.3 %copy-start.2 = (f32[1,2,128,128]{2,3,1,0:T(8,128)}, f32[1,2,128,128]{2,3,1,0:T(8,128)S(1)}, u32[]{:S(2)}) copy-start(f32[1,2,128,128]{2,3,1,0:T(8,128)S(1)} %custom-call.24) | copy-start | bytes 393220
  186.9 129.1 %reduce-scatter.2.cloned.1.call-start = ((), (), s32[]{:S(2)}) async-start(), calls=%async_computation.2 | async-start | bytes 2621440 | tf_op jit(solution)/shard_map/reduce_scatter | solution.py:46
  314.4 1.7 copy-start.3
  316.1 4.4 %copy-start = (f32[1,256,512]{2,1,0:T(8,128)S(1)}, f32[1,256,512]{2,1,0:T(8,128)}, u32[]{:S(2)}) copy-start(f32[1,256,512]{2,1,0:T(8,128)} %reduce-scatter.2.cloned.1.call-done) | copy-start | bytes 1572868
Sparse Core Ops, SparseCore 0:
  14.3 90.1 all-gather.2
  187.0 43.0 all-reduce.3
  233.1 35.3 reduce-scatter.1
